TPU v7x, 32 devices: a whole 2x2x4 slice. The times are simulated.
32 devices in a mesh: seq: 4 (over y, core), fsdp: 8 (over z, x).
Axes of the slice: x: 2, y: 2, z: 4, core: 2. Of those that a mesh axis runs over, the one named last changes fastest.
Arguments:
- tokens: bfloat16 [8, 1024, 2048], P('fsdp', 'seq'), may hold values from -6 to 6
- teacher: bfloat16 [8, 1024, 2048], P('fsdp', 'seq'), may hold values from -6 to 6
- segments: int32 [8, 1024], P('fsdp'), may hold values from 0 to 3, never falling along the last dimension, each value on 1 to 512 neighbouring positions
- valid: int32 [8, 1024], P('fsdp', 'seq'), may hold values from 0 to 1, as said below
- ln1_gain: bfloat16 [2048], P('fsdp'), may hold values from 0.099609375 to 1.8984375
- ln1_bias: bfloat16 [2048], P('fsdp'), may hold values from -1.75 to 1.75
- w_qkv: bfloat16 [2048, 6144], P('fsdp'), may hold values from -0.125 to 0.125
- b_qkv: bfloat16 [6144], P('fsdp'), may hold values from -1.75 to 1.75
- w_out: bfloat16 [2048, 2048], P('fsdp'), may hold values from -0.5 to 0.5
- ln2_gain: bfloat16 [2048], P('fsdp'), may hold values from 0.099609375 to 1.8984375
- ln2_bias: bfloat16 [2048], P('fsdp'), may hold values from -1.75 to 1.75
- w_gate_up: bfloat16 [5632, 2, 2048], P('fsdp'), may hold values from -0.125 to 0.125
- w_down: bfloat16 [5632, 2048], P('fsdp'), may hold values from -0.15625 to 0.15625
Outputs:
- layer_out: bfloat16 [8, 1024, 2048], P('fsdp', 'seq')
- loss: float32 [], replicated
- grad_tokens: bfloat16 [8, 1024, 2048], P('fsdp', 'seq')
- grad_ln1_gain: float32 [2048], P('fsdp')
- grad_ln1_bias: float32 [2048], P('fsdp')
- grad_w_qkv: float32 [2048, 6144], P('fsdp')
- grad_b_qkv: float32 [6144], P('fsdp')
- grad_w_out: float32 [2048, 2048], P('fsdp')
- grad_ln2_gain: float32 [2048], P('fsdp')
- grad_ln2_bias: float32 [2048], P('fsdp')
- grad_w_gate_up: float32 [5632, 2, 2048], P('fsdp')
- grad_w_down: float32 [5632, 2048], P('fsdp')
Inputs may be any that keep to these rules, and one draw needn't show every extreme that they name: `segments`: segment numbers start at 0 in each sequence and never fall; each document has 1 to 512 tokens and one document of each sequence has exactly that many. `valid`: the first token of every sequence counts.
All inputs are finite; a program needn't handle non-finite values.
Results may differ from a plain program's by a relative error of at most 0.01.
Values may be sent and summed in bfloat16 or wider, within the bound.
No kernel may reach another device: no remote copies, remote signals or barrier semaphores. Data moves between devices by JAX's collectives and lax.ppermute only.
A program may use at most 704 MiB of HBM per device.

v0:
```python
import jax
import jax.numpy as jnp
from jax import lax
from jax.sharding import PartitionSpec as P

H = 32
HD = 64
ROT = 16
EPSILON = 1e-05
MASKED_VALUE = -1e30


def norm_parts(values):
    mean_value = jnp.mean(values, axis=-1, keepdims=True)
    centered = values - mean_value
    variance = jnp.mean(centered * centered, axis=-1, keepdims=True)
    inv_std = lax.rsqrt(variance + EPSILON)
    return (centered * inv_std, inv_std)


def norm_back(grad_out, normed, inv_std, gain_vec):
    scaled = grad_out * gain_vec
    mean_scaled = jnp.mean(scaled, axis=-1, keepdims=True)
    mean_cross = jnp.mean(scaled * normed, axis=-1, keepdims=True)
    return inv_std * (scaled - mean_scaled - normed * mean_cross)


def doc_positions(segment):
    places = jnp.arange(segment.shape[0], dtype=jnp.int32)
    change = jnp.concatenate([jnp.ones((1,), dtype=bool), segment[1:] != segment[:-1]])
    starts = lax.cummax(jnp.where(change, places, 0), axis=0)
    return places - starts


def rotate(values, positions, turn_sign):
    half_rot = ROT // 2
    inverse = 10000.0 ** (-(jnp.arange(half_rot, dtype=jnp.float32) * 2.0) / ROT)
    angles = positions.astype(jnp.float32)[:, None] * inverse[None, :]
    cosine = jnp.cos(angles)[:, None, :]
    sine_part = turn_sign * jnp.sin(angles)[:, None, :]
    front_half = values[..., :half_rot]
    back_half = values[..., half_rot:ROT]
    return jnp.concatenate(
        [
            front_half * cosine - back_half * sine_part,
            back_half * cosine + front_half * sine_part,
            values[..., ROT:],
        ],
        axis=-1,
    )


def gate_backward(gate_up, hidden_grad):
    gate_part = gate_up[:, 0]
    up_part = gate_up[:, 1]
    gate_sig = jax.nn.sigmoid(gate_part)
    up_grad = hidden_grad * (gate_part * gate_sig)
    silu_grad = hidden_grad * up_part
    gate_grad = silu_grad * gate_sig + silu_grad * gate_part * gate_sig * (1.0 - gate_sig)
    return jnp.stack([gate_grad, up_grad], axis=1).astype(jnp.bfloat16)


def block_scores(query_block, key_rows, block_seg, segment, first_row, score_scale):
    block_size = query_block.shape[0]
    places = jnp.arange(segment.shape[0], dtype=jnp.int32)
    block_places = first_row + jnp.arange(block_size, dtype=jnp.int32)
    allowed = (block_seg[:, None] == segment[None, :]) & (block_places[:, None] >= places[None, :])
    scores = (
        jnp.einsum("bhd,lhd->hbl", query_block, key_rows, preferred_element_type=jnp.float32)
        * score_scale
    )
    return jnp.where(allowed[None], scores, MASKED_VALUE)


def attention_forward(query_rows, key_rows, value_rows, segment, block_size, score_scale):
    length_total = key_rows.shape[0]

    def one_block(unused, first_row):
        query_block = lax.dynamic_slice_in_dim(query_rows, first_row, block_size, 0)
        block_seg = lax.dynamic_slice_in_dim(segment, first_row, block_size, 0)
        scores = block_scores(query_block, key_rows, block_seg, segment, first_row, score_scale)
        row_max = jnp.max(scores, axis=-1, keepdims=True)
        exp_scores = jnp.exp(scores - row_max)
        row_sum = jnp.sum(exp_scores, axis=-1, keepdims=True)
        probs = (exp_scores / row_sum).astype(jnp.bfloat16)
        block_out = jnp.einsum(
            "hbl,lhd->bhd", probs, value_rows, preferred_element_type=jnp.float32
        )
        return (unused, (block_out.astype(jnp.bfloat16), (row_max + jnp.log(row_sum))[..., 0]))

    firsts = jnp.arange(length_total // block_size, dtype=jnp.int32) * block_size
    unused, (block_outs, log_totals) = lax.scan(one_block, jnp.zeros((), jnp.int32), firsts)
    return (block_outs.reshape(length_total, query_rows.shape[1], query_rows.shape[2]), log_totals)


def attention_backward(
    query_rows, key_rows, value_rows, out_grad, log_totals, segment, block_size, score_scale
):
    length_total = key_rows.shape[0]

    def one_block(grad_carry, block_inputs):
        key_grad, value_grad = grad_carry
        first_row, block_log = block_inputs
        query_block = lax.dynamic_slice_in_dim(query_rows, first_row, block_size, 0)
        grad_block = lax.dynamic_slice_in_dim(out_grad, first_row, block_size, 0)
        block_seg = lax.dynamic_slice_in_dim(segment, first_row, block_size, 0)
        scores = block_scores(query_block, key_rows, block_seg, segment, first_row, score_scale)
        probs = jnp.exp(scores - block_log[..., None])
        prob_low = probs.astype(jnp.bfloat16)
        value_grad = value_grad + jnp.einsum(
            "hbl,bhd->lhd", prob_low, grad_block, preferred_element_type=jnp.float32
        )
        prob_grad = jnp.einsum(
            "bhd,lhd->hbl", grad_block, value_rows, preferred_element_type=jnp.float32
        )
        row_dot = jnp.sum(probs * prob_grad, axis=-1, keepdims=True)
        score_grad = (probs * (prob_grad - row_dot)).astype(jnp.bfloat16)
        query_grad = (
            jnp.einsum("hbl,lhd->bhd", score_grad, key_rows, preferred_element_type=jnp.float32)
            * score_scale
        )
        key_grad = (
            key_grad
            + jnp.einsum(
                "hbl,bhd->lhd", score_grad, query_block, preferred_element_type=jnp.float32
            )
            * score_scale
        )
        return ((key_grad, value_grad), query_grad)

    firsts = jnp.arange(length_total // block_size, dtype=jnp.int32) * block_size
    zero_grad = jnp.zeros(key_rows.shape, jnp.float32)
    (key_grad, value_grad), query_grads = lax.scan(
        one_block, (zero_grad, zero_grad), (firsts, log_totals)
    )
    return (query_grads.reshape(key_rows.shape), key_grad, value_grad)


def reduce_rows(term_rows, row_share):
    return lax.psum_scatter(
        term_rows(jnp.int32(0), row_share * lax.axis_size("fsdp")).astype(jnp.bfloat16),
        "fsdp",
        scatter_dimension=0,
        tiled=True,
    ).astype(jnp.float32)


def per_device(
    tokens,
    teacher,
    segments,
    valid,
    ln1_gain,
    ln1_bias,
    w_qkv,
    b_qkv,
    w_out,
    ln2_gain,
    ln2_bias,
    w_gate_up,
    w_down,
):
    seq_count = lax.axis_size("seq")
    fsdp_count = lax.axis_size("fsdp")
    seq_index = lax.axis_index("seq")
    fsdp_index = lax.axis_index("fsdp")
    row_count = tokens.shape[1]
    model_width = tokens.shape[2]
    length_total = segments.shape[1]
    heads_here = H // seq_count
    group_width = heads_here * HD
    block_size = min(512, length_total)
    score_scale = HD ** (-0.5)
    tokens_total = row_count * seq_count * fsdp_count
    full_qkv, full_out, full_bias, gain_one, shift_one, gain_two, shift_two = (
        lax.all_gather(w_qkv, "fsdp", axis=0, tiled=True),
        lax.all_gather(w_out, "fsdp", axis=0, tiled=True),
        lax.all_gather(b_qkv, "fsdp", axis=0, tiled=True),
        lax.all_gather(ln1_gain, "fsdp", axis=0, tiled=True),
        lax.all_gather(ln1_bias, "fsdp", axis=0, tiled=True),
        lax.all_gather(ln2_gain, "fsdp", axis=0, tiled=True),
        lax.all_gather(ln2_bias, "fsdp", axis=0, tiled=True),
    )
    gain_one = gain_one.astype(jnp.float32)
    gain_two = gain_two.astype(jnp.float32)
    segment = segments[0]
    positions_all = doc_positions(segment)
    positions = lax.dynamic_slice_in_dim(positions_all, seq_index * row_count, row_count, 0)
    tokens_in = tokens[0].astype(jnp.float32)
    teacher_in = teacher[0].astype(jnp.float32)
    counted = valid[0].astype(jnp.float32)
    normed_one, inv_std_one = norm_parts(tokens_in)
    hidden_one = (normed_one * gain_one + shift_one.astype(jnp.float32)).astype(jnp.bfloat16)
    qkv_float = jnp.dot(
        hidden_one, full_qkv, preferred_element_type=jnp.float32
    ) + full_bias.astype(jnp.float32)
    split_rows = qkv_float.reshape(row_count, 3, H, HD)
    packed = jnp.stack(
        [
            rotate(split_rows[:, 0], positions, 1.0),
            rotate(split_rows[:, 1], positions, 1.0),
            split_rows[:, 2],
        ],
        axis=1,
    )
    packed = packed.astype(jnp.bfloat16).reshape(row_count, 3, seq_count, group_width)
    spread = lax.all_to_all(packed, "seq", split_axis=2, concat_axis=0, tiled=True)
    head_rows = spread.reshape(length_total, 3, heads_here, HD)
    query_rows = head_rows[:, 0]
    key_rows = head_rows[:, 1]
    value_rows = head_rows[:, 2]
    heads_out, log_totals = attention_forward(
        query_rows, key_rows, value_rows, segment, block_size, score_scale
    )
    returned = lax.all_to_all(
        heads_out.reshape(length_total, 1, group_width),
        "seq",
        split_axis=0,
        concat_axis=1,
        tiled=True,
    )
    attn_rows = returned.reshape(row_count, model_width)
    resid = tokens_in + jnp.dot(attn_rows, full_out, preferred_element_type=jnp.float32)
    normed_two, inv_std_two = norm_parts(resid)
    hidden_two = (normed_two * gain_two + shift_two.astype(jnp.float32)).astype(jnp.bfloat16)
    piece_gate = lax.all_gather(w_gate_up, "fsdp", axis=0, tiled=True)
    piece_down = lax.all_gather(w_down, "fsdp", axis=0, tiled=True)
    gate_up = jnp.einsum("td,ukd->tku", hidden_two, piece_gate, preferred_element_type=jnp.float32)
    hidden_piece = (jax.nn.silu(gate_up[:, 0]) * gate_up[:, 1]).astype(jnp.bfloat16)
    running = jnp.dot(hidden_piece, piece_down, preferred_element_type=jnp.float32)
    outputs = resid + running
    differ = outputs - teacher_in
    cot = counted[:, None] * differ
    half_sum = 0.5 * jnp.sum(cot * differ)
    count_here = jnp.sum(counted)
    cot_low = cot.astype(jnp.bfloat16)
    piece_gate = lax.all_gather(w_gate_up, "fsdp", axis=0, tiled=True)
    piece_down = lax.all_gather(w_down, "fsdp", axis=0, tiled=True)
    hidden_grad = jnp.einsum("tc,uc->tu", cot_low, piece_down, preferred_element_type=jnp.float32)
    piece_grads = gate_backward(gate_up, hidden_grad)
    grad_running = jnp.einsum(
        "tku,ukd->td", piece_grads, piece_gate, preferred_element_type=jnp.float32
    )

    def unit_rows(first_row, row_total):
        gate_term = jnp.einsum(
            "tku,td->ukd", piece_grads, hidden_two, preferred_element_type=jnp.float32
        )
        down_term = jnp.einsum(
            "tu,td->ud", hidden_piece, cot_low, preferred_element_type=jnp.float32
        )
        return jnp.concatenate([gate_term, down_term[:, None]], axis=1)

    ff_shard = reduce_rows(unit_rows, w_down.shape[0])
    resid_grad = cot + norm_back(grad_running, normed_two, inv_std_two, gain_two)
    gain_two_grad = jnp.sum(grad_running * normed_two, axis=0)
    shift_two_grad = jnp.sum(grad_running, axis=0)
    resid_low = resid_grad.astype(jnp.bfloat16)
    out_grad = jnp.einsum(
        "tc,ec->te", resid_low, full_out, preferred_element_type=jnp.float32
    ).astype(jnp.bfloat16)
    head_grad = lax.all_to_all(
        out_grad.reshape(row_count, seq_count, group_width),
        "seq",
        split_axis=1,
        concat_axis=0,
        tiled=True,
    )
    head_grad = head_grad.reshape(length_total, heads_here, HD)
    query_grad, key_grad, value_grad = attention_backward(
        query_rows, key_rows, value_rows, head_grad, log_totals, segment, block_size, score_scale
    )
    back_packed = jnp.stack(
        [
            rotate(query_grad, positions_all, -1.0),
            rotate(key_grad, positions_all, -1.0),
            value_grad,
        ],
        axis=1,
    )
    back_packed = back_packed.astype(jnp.bfloat16).reshape(length_total, 3, 1, group_width)
    qkv_grad = lax.all_to_all(back_packed, "seq", split_axis=0, concat_axis=2, tiled=True).reshape(
        row_count, 3 * model_width
    )
    grad_one = jnp.einsum("tc,ec->te", qkv_grad, full_qkv, preferred_element_type=jnp.float32)
    tokens_grad = resid_grad + norm_back(grad_one, normed_one, inv_std_one, gain_one)
    gain_one_grad = jnp.sum(grad_one * normed_one, axis=0)
    shift_one_grad = jnp.sum(grad_one, axis=0)
    bias_grad = jnp.sum(qkv_grad.astype(jnp.float32), axis=0)

    def feature_rows(first_row, row_total):
        qkv_term = jnp.einsum("tr,tc->rc", hidden_one, qkv_grad, preferred_element_type=jnp.float32)
        out_term = jnp.einsum("tr,tc->rc", attn_rows, resid_low, preferred_element_type=jnp.float32)
        return jnp.concatenate([qkv_term, out_term], axis=1)

    attn_shard = reduce_rows(feature_rows, w_qkv.shape[0])
    attn_total, ff_total = (
        lax.psum(attn_shard.astype(jnp.bfloat16), "seq").astype(jnp.float32),
        lax.psum(ff_shard.astype(jnp.bfloat16), "seq").astype(jnp.float32),
    )
    (
        sum_half,
        sum_count,
        total_gain_one,
        total_shift_one,
        total_gain_two,
        total_shift_two,
        total_bias,
    ) = lax.psum(
        (
            half_sum,
            count_here,
            gain_one_grad,
            shift_one_grad,
            gain_two_grad,
            shift_two_grad,
            bias_grad,
        ),
        ("seq", "fsdp"),
    )
    factor = tokens_total / sum_count
    loss = 2.0 * sum_half / (sum_count * model_width)

    def own_part(total_vec):
        share = total_vec.shape[0] // fsdp_count
        return factor * lax.dynamic_slice_in_dim(total_vec, fsdp_index * share, share, 0)

    layer_out = outputs.astype(jnp.bfloat16)[None]
    grad_tokens = (factor * tokens_grad).astype(jnp.bfloat16)[None]
    return (
        layer_out,
        loss,
        grad_tokens,
        own_part(total_gain_one),
        own_part(total_shift_one),
        factor * attn_total[:, : 3 * model_width],
        own_part(total_bias),
        factor * attn_total[:, 3 * model_width :],
        own_part(total_gain_two),
        own_part(total_shift_two),
        factor * ff_total[:, :2],
        factor * ff_total[:, 2],
    )


def solution(mesh):
    placed = (
        P("fsdp", "seq", None),
        P("fsdp", "seq", None),
        P("fsdp", None),
        P("fsdp", "seq"),
        P("fsdp"),
        P("fsdp"),
        P("fsdp", None),
        P("fsdp"),
        P("fsdp", None),
        P("fsdp"),
        P("fsdp"),
        P("fsdp", None, None),
        P("fsdp", None),
    )
    return jax.shard_map(
        per_device,
        mesh=mesh,
        in_specs=placed,
        out_specs=(
            P("fsdp", "seq", None),
            P(),
            P("fsdp", "seq", None),
            P("fsdp"),
            P("fsdp"),
            P("fsdp", None),
            P("fsdp"),
            P("fsdp", None),
            P("fsdp"),
            P("fsdp"),
            P("fsdp", None, None),
            P("fsdp", None),
        ),
        check_vma=False,
    )
```

profile of v0, /device:TPU:0, one launch (start us, length us, event | category | flops | bytes accessed | tf_op | source)
XLA Modules:
  0.0 4082.9 jit_solution(5188963605835579992)
XLA Ops:
  17.8 48.8 %all-gather.1 = bf16[8,1,256]{2,1,0:T(2,128)(2,1)S(1)} all-gather(bf16[1,1,256]{2,1,0:T(2,128)(2,1)S(1)} %reshape.465), channel_id=1, replica_groups=mesh['seq'=4,'fsdp'=8] {'fsdp'}, dimensions={0}, use_global_device_ids=true | all-gather | bytes 4608 | tf_op jit(solution)/shard_map/all_gather | solution.py:180
  66.6 30.9 all-gather
  97.5 39.9 all-gather.2
  139.2 354.2 %all-gather.10.cloned.1.call-done = bf16[2048,6144]{1,0:T(8,128)(2,1)} async-done(((bf16[256,6144]{1,0:T(8,128)(2,1)}), bf16[2048,6144]{1,0:T(8,128)(2,1)}) %all-gather.10.cloned.1.call-update) | async-done | bytes 25165840 | tf_op jit(solution)/shard_map/all_gather | solution.py:176
  493.4 13.4 convolution_add_fusion
  524.5 36.8 all-to-all-done
  575.3 37.4 while.27
  638.5 64.3 %all-gather.4 = bf16[8,1,256]{2,1,0:T(2,128)(2,1)S(1)} all-gather(bf16[1,1,256]{2,1,0:T(2,128)(2,1)S(1)} %reshape.471), channel_id=1, replica_groups=mesh['seq'=4,'fsdp'=8] {'fsdp'}, dimensions={0}, use_global_device_ids=true | all-gather | bytes 4608 | tf_op jit(solution)/shard_map/all_gather | solution.py:182
  702.8 30.6 all-gather.3
  745.9 748.3 %all-gather.14.cloned.1.call-done = bf16[5632,2,2048]{2,0,1:T(8,128)(2,1)} async-done(((bf16[704,2,2048]{2,0,1:T(8,128)(2,1)}), bf16[5632,2,2048]{2,0,1:T(8,128)(2,1)}) %all-gather.14.cloned.1.call-update) | async-done | bytes 46137360 | tf_op jit(solution)/shard_map/all_gather | solution.py:226
  1494.3 23.7 convolution_bitcast_fusion
  1524.3 412.4 %all-gather.16.cloned.1.call-done = bf16[5632,2048]{1,0:T(8,128)(2,1)} async-done(((bf16[704,2048]{1,0:T(8,128)(2,1)}), bf16[5632,2048]{1,0:T(8,128)(2,1)}) %all-gather.16.cloned.1.call-update) | async-done | bytes 23068688 | tf_op jit(solution)/shard_map/all_gather | solution.py:227
  1961.9 25.6 fusion.31
  1987.4 21.2 convert_bitcast_fusion
  2008.6 46.8 %pad_maximum_fusion = bf16[5632,3,2048]{0,2,1:T(8,128)(2,1)} fusion(bf16[5632,1,2048]{0,2,1:T(8,128)(2,1)} %convert_bitcast_fusion.1, bf16[5632,2,2048]{0,2,1:T(8,128)(2,1)} %convert_bitcast_fusion), kind=kLoop, calls=%fused_computation.40 | loop fusion | flops 34603008 | bytes 138412032 | tf_op jit(solution)/shard_map/concatenate | solution.py:252
  2055.4 88.8 %copy.142 = bf16[5632,6144]{1,0:T(8,128)(2,1)} copy(bf16[5632,6144]{0,1:T(8,128)(2,1)} %bitcast.64) | data formatting | bytes 138412032
  2144.3 22.0 multiply_reduce_fusion.1
  2181.6 13.5 all-to-all-done.2
  2197.4 154.1 %while.28 = (s32[]{:T(128)}, f32[1024,8,64]{0,2,1:T(8,128)}, f32[1024,8,64]{0,2,1:T(8,128)}, f32[2,512,8,64]{1,0,3,2:T(2,128)}, s32[2]{0:T(128)S(1)}, /*index=5*...) while((s32[]{:T(128)}, f32[1024,8,64]{0,2,1:T(8,128)}, ...), condition=%wide.region_18.19_spmd.clone, body=%wide.region_16.18_spmd.clone.sunk | while | flops 2726556160 | bytes 233929072 | solution.py:133
  2211.3 13.8 multiply_reduce_fusion.7
  2254.5 19.7 dynamic_update_slice.20
  2287.8 13.9 multiply_reduce_fusion.7
  2331.7 19.6 dynamic_update_slice.20
  2376.5 42.4 %all-to-all-done.3 = bf16[1024,3,1,512]{3,1,2,0:T(4,128)(2,1)} async-done(((bf16[1024,3,1,512]{3,1,2,0:T(4,128)(2,1)}), bf16[1024,3,1,512]{3,1,2,0:T(4,128)(2,1)}, u32[]{:S(2)}, u32[]{:S(2)}) %all-to-all-start.3) | async-done | bytes 3145760 | tf_op jit(solution)/shard_map/all_to_all | solution.py:282
  2428.5 14.3 convolution_convert_fusion
  2442.9 22.9 pad_maximum_fusion.1
  2465.8 764.0 %reduce-scatter.7.cloned.1.call-done = bf16[704,6144]{1,0:T(8,128)(2,1)} async-done(((bf16[5632,6144]{1,0:T(8,128)(2,1)}), bf16[704,6144]{1,0:T(8,128)(2,1)}) %reduce-scatter.7.cloned.1.call-update) | async-done | bytes 8650768
  3242.6 529.5 %reduce-scatter.5.cloned.1.call-done = bf16[256,8192]{1,0:T(8,128)(2,1)} async-done(((bf16[2048,8192]{1,0:T(8,128)(2,1)}), bf16[256,8192]{1,0:T(8,128)(2,1)}) %reduce-scatter.5.cloned.1.call-update) | async-done | bytes 4194320 | tf_op jit(solution)/shard_map/reduce_scatter | solution.py:140
  3776.4 15.2 fusion.49
  3791.6 41.5 %all-reduce = (f32[]{:T(128)}, f32[]{:T(128)}, f32[2048]{0:T(1024)S(1)}, f32[2048]{0:T(1024)S(1)}, f32[6144]{0:T(1024)S(1)}, /*index=5*/f32[2048]{0:T(1024)S(1)}, f32[2048]{0:T(1024)S(1)}) all-reduce(f32[]{:T(128)S(6)} %mul_shard_map.3, f32[]{:T(128)} %convert_reduce_fusion.2, ...), channel_id=1, replica_groups=mesh['seq'=4,'fsdp'=8] {'seq','fsdp'}, use_global_device_ids=true, to_apply=%region_11.12 | all-reduce | flops 14338 | bytes 114704 | tf_op jit(solution)/shard_map/psum | solution.py:309
  3841.8 171.7 %all-reduce.4.cloned.1.call-done = (bf16[256,8192]{1,0:T(8,128)(2,1)}, bf16[704,3,2048]{0,2,1:T(8,128)(2,1)}) async-done(((bf16[256,8192]{1,0:T(8,128)(2,1)}, bf16[704,3,2048]{0,2,1:T(8,128)(2,1)}), (bf16[256,8192]{1,0:T(8,128)(2,1)}, bf16[704,3,2048]{0,2,1:T(8,128)(2,1)})) %all-reduce.4.cloned.1.call-update) | async-done | bytes 12845072 | tf_op jit(solution)/shard_map/psum | solution.py:298
  4049.0 19.1 copy.132
  (260 shorter events, 346.7 us)
Async XLA Ops:
  7.2 486.2 %all-gather.10.cloned.1.call-start = ((), (), s32[]{:S(2)}) async-start(), calls=%async_computation.6 | async-start | bytes 28311552 | tf_op jit(solution)/shard_map/all_gather | solution.py:176
  7.9 731.3 %all-gather.12.cloned.1.call-start = ((), (), s32[]{:S(2)}) async-start(), calls=%async_computation.7 | async-start | bytes 9437184 | tf_op jit(solution)/shard_map/all_gather | solution.py:177
  8.7 1485.6 %all-gather.14.cloned.1.call-start = ((), (), s32[]{:S(2)}) async-start(), calls=%async_computation.8 | async-start | bytes 51904512 | tf_op jit(solution)/shard_map/all_gather | solution.py:226
  16.5 121.9 %copy-start.8 = (bf16[1,256,2048]{2,1,0:T(8,128)(2,1)S(1)}, bf16[1,256,2048]{2,1,0:T(8,128)(2,1)}, u32[]{:S(2)}) copy-start(bf16[1,256,2048]{2,1,0:T(8,128)(2,1)} %param.17) | copy-start | bytes 3145732
  16.6 1920.1 %all-gather.16.cloned.1.call-start = ((), (), s32[]{:S(2)}) async-start(), calls=%async_computation.9 | async-start | bytes 25952256 | tf_op jit(solution)/shard_map/all_gather | solution.py:227
  66.6 440.2 %copy-start.22 = (f32[8,1,256]{2,1,0:T(1,128)}, f32[8,1,256]{2,1,0:T(1,128)S(1)}, u32[]{:S(2)}) copy-start(f32[8,1,256]{2,1,0:T(1,128)S(1)} %convert_element_type.149) | copy-start | bytes 24580
  97.5 409.3 %copy-start.20 = (f32[8,1,256]{2,1,0:T(1,128)}, f32[8,1,256]{2,1,0:T(1,128)S(1)}, u32[]{:S(2)}) copy-start(f32[8,1,256]{2,1,0:T(1,128)S(1)} %convert_element_type.148) | copy-start | bytes 24580
  137.5 369.3 %copy-start.37 = (f32[8]{0:T(128)}, f32[8]{0:T(128)S(1)}, u32[]{:S(2)}) copy-start(f32[8]{0:T(128)S(1)} %multiply_power_fusion) | copy-start | bytes 100
  138.6 368.2 %copy-start.28 = (f32[256]{0:T(256)}, f32[256]{0:T(256)S(1)}, u32[]{:S(2)}) copy-start(f32[256]{0:T(256)S(1)} %broadcast_multiply_fusion.5) | copy-start | bytes 3076
  139.0 367.8 %copy-start.30 = (f32[256]{0:T(256)}, f32[256]{0:T(256)S(1)}, u32[]{:S(2)}) copy-start(f32[256]{0:T(256)S(1)} %add_rsqrt_fusion.1) | copy-start | bytes 3076
  520.6 40.8 all-to-all-start
  612.8 125.1 %copy-start.1 = (bf16[1024,8,64]{0,2,1:T(8,128)(2,1)}, bf16[1024,8,64]{0,2,1:T(8,128)(2,1)S(1)}, u32[]{:S(2)}) copy-start(bf16[1024,8,64]{0,2,1:T(8,128)(2,1)S(1)} %get-tuple-element.590) | copy-start | bytes 3145732
  623.0 15.5 copy-start.40
  634.8 98.6 %all-to-all-start.1 = ((bf16[4,2,65536]{2,1,0:T(2,128)(2,1)}), bf16[4,2,65536]{2,1,0:T(2,128)(2,1)S(1)}, u32[]{:S(2)}, u32[]{:S(2)}) async-start(bf16[4,2,65536]{2,1,0:T(2,128)(2,1)} %reshape.486), calls=%async_computation.1 | async-start | bytes 2097152 | tf_op jit(solution)/shard_map/all_to_all | solution.py:215
  638.4 2591.4 %reduce-scatter.7.cloned.1.call-start = ((), (), s32[]{:S(2)}) async-start(), calls=%async_computation.11 | async-start | bytes 77856768
  638.5 1298.2 %copy-start.35 = (f32[1,256]{1,0:T(1,128)}, f32[1,256]{1,0:T(1,128)S(1)}, u32[]{:S(2)}) copy-start(f32[1,256]{1,0:T(1,128)S(1)} %convert_element_type.133) | copy-start | bytes 3076
  1518.0 418.7 %copy-start.17 = (bf16[1,256,2048]{2,1,0:T(8,128)(2,1)S(1)}, bf16[1,256,2048]{2,1,0:T(8,128)(2,1)}, u32[]{:S(2)}) copy-start(bf16[1,256,2048]{2,1,0:T(8,128)(2,1)} %param.18) | copy-start | bytes 3145732
  2144.2 22.0 copy-start.14
  2144.2 22.0 copy-start.18
  2144.3 22.0 copy-start.36
  2177.1 20.3 copy-start.2
  2177.1 20.3 copy-start.16
  2177.1 20.3 copy-start.25
  2177.1 20.3 copy-start.47
  2177.1 18.1 all-to-all-start.2
  2225.1 15.9 copy-start
  2253.4 20.7 copy-start.3
  2301.7 15.8 copy-start
  2330.6 20.7 copy-start.3
  2365.6 53.3 %all-to-all-start.3 = ((bf16[1024,3,1,512]{3,1,2,0:T(4,128)(2,1)}), bf16[1024,3,1,512]{3,1,2,0:T(4,128)(2,1)}, u32[]{:S(2)}, u32[]{:S(2)}) async-start(bf16[1024,3,1,512]{3,1,2,0:T(4,128)(2,1)} %copy.126), calls=%async_computation.3 | async-start | bytes 8388608 | tf_op jit(solution)/shard_map/all_to_all | solution.py:282
  2370.7 1401.4 %reduce-scatter.5.cloned.1.call-start = ((), (), s32[]{:S(2)}) async-start(), calls=%async_computation.10 | async-start | bytes 37748736 | tf_op jit(solution)/shard_map/reduce_scatter | solution.py:140
  2465.8 1547.7 %all-reduce.4.cloned.1.call-start = ((), (), s32[]{:S(2)}) async-start(), calls=%async_computation.12 | async-start | bytes 27262976 | tf_op jit(solution)/shard_map/psum | solution.py:298
  (31 other events, 163.8 us)
Sparse Core Ops, SparseCore 0:
  9.5 483.8 all-gather.9
  495.5 124.4 all-gather.11
  622.1 872.0 all-gather.13
  1495.6 441.0 all-gather.15
  2144.4 1085.4 reduce-scatter.6
  3233.5 538.6 reduce-scatter.4
  3775.3 238.1 all-reduce.3
where the time goes:
time: 4100 us; the launch traced here: 4080 us
  waiting for transfers between devices  3070 us (75%)
  matrix products  270 us (7%)
  local copies, waits for them, and re-layouts  262 us (6%)
  blocking collectives  256 us (6%)
  other arithmetic  175 us (4%)
    unnamed x8, waiting for transfers between devices  766 us
    all_gather x1, waiting for transfers between devices, per_device(): piece_gate = lax.all_gather(w_gate_up, 'fsdp', axis=0, tiled=True)  748 us
    reduce_scatter x1, waiting for transfers between devices, reduce_rows(): lax.psum_scatter(term_rows(jnp.int32(0), row_share * lax.axis_size('fsdp'...  530 us
    all_gather x1, waiting for transfers between devices, per_device(): piece_down = lax.all_gather(w_down, 'fsdp', axis=0, tiled=True)  412 us
    all_gather x1, waiting for transfers between devices, per_device(): lax.all_gather(w_qkv, 'fsdp', axis=0, tiled=True)  354 us
    psum x1, waiting for transfers between devices, per_device(): lax.psum(attn_shard.astype(jnp.bfloat16), 'seq').astype(jnp.float32)  172 us
    unnamed x102, local copies, waits for them, and re-layouts  144 us
  transfers between devices with their start and end apart: 11, of which 9 were waited for; matrix products, arithmetic and copies ran while one was open for 10% of the time, Pallas kernels for 0%

commit v1 on v0

--- a/solution.py
+++ b/solution.py
@@ -224,7 +224,37 @@
     normed_two, inv_std_two = norm_parts(resid)
     hidden_two = (normed_two * gain_two + shift_two.astype(jnp.float32)).astype(jnp.bfloat16)
     piece_gate = lax.all_gather(w_gate_up, "fsdp", axis=0, tiled=True)
-    piece_down = lax.all_gather(w_down, "fsdp", axis=0, tiled=True)
+
+    def table_replace(link_axis, array_here):
+        current_block = lax.axis_size(link_axis)
+        known = lax.axis_index(link_axis)
+        mid_arr, front, passed = (current_block, known, array_here.shape[0])
+        r_now = jnp.zeros(
+            [p * mid_arr if u == 0 else p for u, p in enumerate(array_here.shape)], array_here.dtype
+        )
+        block_next = lax.dynamic_update_slice_in_dim(r_now, array_here, front * passed, axis=0)
+        long_array = d_next = array_here
+        for rr in range(1, mid_arr // 2 + 1):
+            long_array = lax.ppermute(
+                long_array,
+                axis_name=link_axis,
+                perm=[(u, (u + 1) % mid_arr) for u in range(mid_arr)],
+            )
+            block_next = lax.dynamic_update_slice_in_dim(
+                block_next, long_array, (front - rr) % mid_arr * passed, axis=0
+            )
+            if 2 * rr < mid_arr:
+                d_next = lax.ppermute(
+                    d_next,
+                    axis_name=link_axis,
+                    perm=[(u, (u - 1) % mid_arr) for u in range(mid_arr)],
+                )
+                block_next = lax.dynamic_update_slice_in_dim(
+                    block_next, d_next, (front + rr) % mid_arr * passed, axis=0
+                )
+        return block_next
+
+    piece_down = table_replace("fsdp", w_down)
     gate_up = jnp.einsum("td,ukd->tku", hidden_two, piece_gate, preferred_element_type=jnp.float32)
     hidden_piece = (jax.nn.silu(gate_up[:, 0]) * gate_up[:, 1]).astype(jnp.bfloat16)
     running = jnp.dot(hidden_piece, piece_down, preferred_element_type=jnp.float32)

time: 4100 us -> 4480 us (1.093)
  blocking collectives: 256 us -> 458 us
  waiting for transfers between devices: 3070 us -> 3200 us
    ppermute x0 -> x7, waiting for transfers between devices: none -> 395 us  [the longest x4 274 us: table_replace(): lax.ppermute(long_array, axis_name=link_axis, perm=[(u, (u + 1) % mid_arr...]
    all_gather x1, waiting for transfers between devices: 354 us -> 135 us  [per_device(): lax.all_gather(w_qkv, 'fsdp', axis=0, tiled=True)]
    all_gather x1, blocking collectives: 39.9 us -> 199 us  [per_device(): lax.all_gather(b_qkv, 'fsdp', axis=0, tiled=True)]
    all_gather x1, blocking collectives: 30.9 us -> 83.4 us  [per_device(): lax.all_gather(ln1_gain, 'fsdp', axis=0, tiled=True)]
    all_gather x1, blocking collectives: 64.3 us -> 18.3 us  [per_device(): lax.all_gather(ln2_bias, 'fsdp', axis=0, tiled=True)]
    unnamed x102 -> x110, local copies, waits for them, and re-layouts: 144 us -> 143 us
  transfers between devices with their start and end apart: 11 -> 18, of which waited for: 9 -> 10; matrix products, arithmetic and copies ran while one was open for 10% -> 11% of each run, Pallas kernels for 0% -> 0%
where the time goes in v1:
time: 4480 us; the launch traced here: 4470 us
  waiting for transfers between devices  3200 us (71%)
  blocking collectives  458 us (10%)
  local copies, waits for them, and re-layouts  292 us (7%)
  matrix products  272 us (6%)
  other arithmetic  186 us (4%)
    all_gather x1, waiting for transfers between devices, per_device(): piece_gate = lax.all_gather(w_gate_up, 'fsdp', axis=0, tiled=True)  774 us
    unnamed x8, waiting for transfers between devices  754 us
    reduce_scatter x1, waiting for transfers between devices, reduce_rows(): lax.psum_scatter(term_rows(jnp.int32(0), row_share * lax.axis_size('fsdp'...  530 us
    all_gather x1, waiting for transfers between devices, per_device(): piece_down = lax.all_gather(w_down, 'fsdp', axis=0, tiled=True)  386 us
    ppermute x4, waiting for transfers between devices, table_replace(): lax.ppermute(long_array, axis_name=link_axis, perm=[(u, (u + 1) % mid_arr...  274 us
    all_gather x1, blocking collectives, per_device(): lax.all_gather(b_qkv, 'fsdp', axis=0, tiled=True)  199 us
    psum x1, waiting for transfers between devices, per_device(): lax.psum(attn_shard.astype(jnp.bfloat16), 'seq').astype(jnp.float32)  172 us
    unnamed x110, local copies, waits for them, and re-layouts  143 us
  transfers between devices with their start and end apart: 18, of which 10 were waited for; matrix products, arithmetic and copies ran while one was open for 11% of the time, Pallas kernels for 0%

profile of v1, /device:TPU:0, one launch (start us, length us, event | category | flops | bytes accessed | tf_op | source)
XLA Modules:
  0.0 4466.8 jit_solution(9015921665729905570)
XLA Ops:
  23.3 274.3 %collective-permute-done = bf16[704,2048]{1,0:T(8,128)(2,1)} collective-permute-done((bf16[704,2048]{1,0:T(8,128)(2,1)}, bf16[704,2048]{1,0:T(8,128)(2,1)}, u32[]{:S(2)}, u32[]{:S(2)}) %collective-permute-start) | collective-permute-done | bytes 2883616 | tf_op jit(solution)/shard_map/ppermute | solution.py:238
  300.1 199.3 %all-gather.2 = bf16[8,1,768]{2,1,0:T(2,128)(2,1)S(1)} all-gather(bf16[1,1,768]{2,1,0:T(2,128)(2,1)S(1)} %reshape.467), channel_id=1, replica_groups=mesh['seq'=4,'fsdp'=8] {'fsdp'}, dimensions={0}, use_global_device_ids=true | all-gather | bytes 13824 | tf_op jit(solution)/shard_map/all_gather | solution.py:178
  499.4 85.1 %all-gather.1 = bf16[8,1,256]{2,1,0:T(2,128)(2,1)S(1)} all-gather(bf16[1,1,256]{2,1,0:T(2,128)(2,1)S(1)} %reshape.465), channel_id=1, replica_groups=mesh['seq'=4,'fsdp'=8] {'fsdp'}, dimensions={0}, use_global_device_ids=true | all-gather | bytes 4608 | tf_op jit(solution)/shard_map/all_gather | solution.py:180
  584.6 83.4 %all-gather = bf16[8,1,256]{2,1,0:T(2,128)(2,1)S(1)} all-gather(bf16[1,1,256]{2,1,0:T(2,128)(2,1)S(1)} %reshape.463), channel_id=1, replica_groups=mesh['seq'=4,'fsdp'=8] {'fsdp'}, dimensions={0}, use_global_device_ids=true | all-gather | bytes 4608 | tf_op jit(solution)/shard_map/all_gather | solution.py:179
  672.4 135.3 %all-gather.10.cloned.1.call-done = bf16[2048,6144]{1,0:T(8,128)(2,1)} async-done(((bf16[256,6144]{1,0:T(8,128)(2,1)}), bf16[2048,6144]{1,0:T(8,128)(2,1)}) %all-gather.10.cloned.1.call-update) | async-done | bytes 25165840 | tf_op jit(solution)/shard_map/all_gather | solution.py:176
  839.0 30.6 all-gather.3
  870.2 18.3 all-gather.4
  930.8 37.4 while.27
  997.5 121.1 %collective-permute-done.5 = bf16[704,2048]{1,0:T(8,128)(2,1)} collective-permute-done((bf16[704,2048]{1,0:T(8,128)(2,1)}, bf16[704,2048]{1,0:T(8,128)(2,1)}, u32[]{:S(2)}, u32[]{:S(2)}) %collective-permute-start.5) | collective-permute-done | bytes 2883616 | tf_op jit(solution)/shard_map/ppermute | solution.py:247
  1137.4 774.5 %all-gather.14.cloned.1.call-done = bf16[5632,2,2048]{2,0,1:T(8,128)(2,1)} async-done(((bf16[704,2,2048]{2,0,1:T(8,128)(2,1)}), bf16[5632,2,2048]{2,0,1:T(8,128)(2,1)}) %all-gather.14.cloned.1.call-update) | async-done | bytes 46137360 | tf_op jit(solution)/shard_map/all_gather | solution.py:226
  1911.8 23.7 convolution_bitcast_fusion
  1968.2 386.1 %all-gather.16.cloned.1.call-done = bf16[5632,2048]{1,0:T(8,128)(2,1)} async-done(((bf16[704,2048]{1,0:T(8,128)(2,1)}), bf16[5632,2048]{1,0:T(8,128)(2,1)}) %all-gather.16.cloned.1.call-update) | async-done | bytes 23068688 | tf_op jit(solution)/shard_map/all_gather | solution.py:268
  2354.3 17.7 fusion.31
  2372.0 21.2 convert_bitcast_fusion
  2393.2 46.3 %pad_maximum_fusion = bf16[5632,3,2048]{0,2,1:T(8,128)(2,1)} fusion(bf16[5632,1,2048]{0,2,1:T(8,128)(2,1)} %convert_bitcast_fusion.1, bf16[5632,2,2048]{0,2,1:T(8,128)(2,1)} %convert_bitcast_fusion), kind=kLoop, calls=%fused_computation.40 | loop fusion | flops 34603008 | bytes 138412032 | tf_op jit(solution)/shard_map/concatenate | solution.py:282
  2439.6 88.8 %copy.142 = bf16[5632,6144]{1,0:T(8,128)(2,1)} copy(bf16[5632,6144]{0,1:T(8,128)(2,1)} %bitcast.64) | data formatting | bytes 138412032
  2528.4 22.0 multiply_reduce_fusion.1
  2581.6 164.2 %while.28 = (s32[]{:T(128)}, f32[1024,8,64]{0,2,1:T(8,128)}, f32[1024,8,64]{0,2,1:T(8,128)}, f32[2,512,8,64]{1,0,3,2:T(2,128)}, s32[2]{0:T(128)S(1)}, /*index=5*...) while((s32[]{:T(128)}, f32[1024,8,64]{0,2,1:T(8,128)}, ...), condition=%wide.region_18.19_spmd.clone, body=%wide.region_16.18_spmd.clone.sunk | while | flops 2726556160 | bytes 242317680 | solution.py:133
  2609.1 15.4 multiply_convert_fusion.5
  2643.2 19.6 dynamic_update_slice.60
  2676.6 13.9 multiply_reduce_fusion.7
  2690.4 15.2 multiply_convert_fusion.5
  2726.0 19.6 dynamic_update_slice.60
  2772.0 42.4 all-to-all-done.3
  2824.0 14.2 convolution_convert_fusion
  2838.1 23.6 pad_maximum_fusion.1
  2861.8 751.9 %reduce-scatter.7.cloned.1.call-done = bf16[704,6144]{1,0:T(8,128)(2,1)} async-done(((bf16[5632,6144]{1,0:T(8,128)(2,1)}), bf16[704,6144]{1,0:T(8,128)(2,1)}) %reduce-scatter.7.cloned.1.call-update) | async-done | bytes 8650768
  3626.5 529.7 %reduce-scatter.5.cloned.1.call-done = bf16[256,8192]{1,0:T(8,128)(2,1)} async-done(((bf16[2048,8192]{1,0:T(8,128)(2,1)}), bf16[256,8192]{1,0:T(8,128)(2,1)}) %reduce-scatter.5.cloned.1.call-update) | async-done | bytes 4194320 | tf_op jit(solution)/shard_map/reduce_scatter | solution.py:140
  4160.5 15.2 fusion.49
  4175.6 41.4 all-reduce
  4225.8 171.7 %all-reduce.4.cloned.1.call-done = (bf16[256,8192]{1,0:T(8,128)(2,1)}, bf16[704,3,2048]{0,2,1:T(8,128)(2,1)}) async-done(((bf16[256,8192]{1,0:T(8,128)(2,1)}, bf16[704,3,2048]{0,2,1:T(8,128)(2,1)}), (bf16[256,8192]{1,0:T(8,128)(2,1)}, bf16[704,3,2048]{0,2,1:T(8,128)(2,1)})) %all-reduce.4.cloned.1.call-update) | async-done | bytes 12845072 | tf_op jit(solution)/shard_map/psum | solution.py:328
  4432.9 19.1 copy.132
  (293 shorter events, 418.5 us)
Async XLA Ops:
  7.2 800.6 %all-gather.10.cloned.1.call-start = ((), (), s32[]{:S(2)}) async-start(), calls=%async_computation.6 | async-start | bytes 28311552 | tf_op jit(solution)/shard_map/all_gather | solution.py:176
  7.9 1122.8 %all-gather.12.cloned.1.call-start = ((), (), s32[]{:S(2)}) async-start(), calls=%async_computation.7 | async-start | bytes 9437184 | tf_op jit(solution)/shard_map/all_gather | solution.py:177
  8.7 1903.2 %all-gather.14.cloned.1.call-start = ((), (), s32[]{:S(2)}) async-start(), calls=%async_computation.8 | async-start | bytes 51904512 | tf_op jit(solution)/shard_map/all_gather | solution.py:226
  16.5 283.6 %copy-start.41 = (bf16[768]{0:T(1024)(128)(2,1)S(1)}, bf16[768]{0:T(1024)(128)(2,1)}, u32[]{:S(2)}) copy-start(bf16[768]{0:T(1024)(128)(2,1)} %param.24) | copy-start | bytes 4612
  16.5 482.9 %copy-start.44 = (bf16[256]{0:T(256)(128)(2,1)S(1)}, bf16[256]{0:T(256)(128)(2,1)}, u32[]{:S(2)}) copy-start(bf16[256]{0:T(256)(128)(2,1)} %param.22) | copy-start | bytes 1540
  16.5 568.1 %copy-start.45 = (bf16[256]{0:T(256)(128)(2,1)S(1)}, bf16[256]{0:T(256)(128)(2,1)}, u32[]{:S(2)}) copy-start(bf16[256]{0:T(256)(128)(2,1)} %param.21) | copy-start | bytes 1540
  16.5 651.6 %copy-start.16 = (s32[1,1024]{1,0:T(1,128)S(1)}, s32[1,1024]{1,0:T(1,128)}, u32[]{:S(2)}) copy-start(s32[1,1024]{1,0:T(1,128)} %param.19) | copy-start | bytes 12292
  16.5 653.0 %copy-start.4 = (bf16[1,256,2048]{2,1,0:T(8,128)(2,1)S(1)}, bf16[1,256,2048]{2,1,0:T(8,128)(2,1)}, u32[]{:S(2)}) copy-start(bf16[1,256,2048]{2,1,0:T(8,128)(2,1)} %param.17) | copy-start | bytes 3145732
  16.6 2337.8 %all-gather.16.cloned.1.call-start = ((), (), s32[]{:S(2)}) async-start(), calls=%async_computation.9 | async-start | bytes 25952256 | tf_op jit(solution)/shard_map/all_gather | solution.py:268
  17.1 280.5 %collective-permute-start = (bf16[704,2048]{1,0:T(8,128)(2,1)}, bf16[704,2048]{1,0:T(8,128)(2,1)}, u32[]{:S(2)}, u32[]{:S(2)}) collective-permute-start(bf16[704,2048]{1,0:T(8,128)(2,1)} %param.29), channel_id=1, source_target_pairs={{0,1},{1,2},{2,3},{3,4},{4,5},{5,6},{6,7},{7,0},{8,9},{9,10},{10,1... | collective-permute-start | bytes 8650760 | tf_op jit(solution)/shard_map/ppermute | solution.py:238
  20.2 650.2 %collective-permute-start.1 = (bf16[704,2048]{1,0:T(8,128)(2,1)}, bf16[704,2048]{1,0:T(8,128)(2,1)}, u32[]{:S(2)}, u32[]{:S(2)}) collective-permute-start(bf16[704,2048]{1,0:T(8,128)(2,1)} %param.29), channel_id=1, source_target_pairs={{0,7},{1,0},{2,1},{3,2},{4,3},{5,4},{6,5},{7,6},{8,15},{9,8},{10,9... | collective-permute-start | bytes 8650760 | tf_op jit(solution)/shard_map/ppermute | solution.py:247
  297.6 372.8 %collective-permute-start.2 = (bf16[704,2048]{1,0:T(8,128)(2,1)}, bf16[704,2048]{1,0:T(8,128)(2,1)}, u32[]{:S(2)}, u32[]{:S(2)}) collective-permute-start(bf16[704,2048]{1,0:T(8,128)(2,1)} %collective-permute-done), channel_id=1, source_target_pairs={{0,1},{1,2},{2,3},{3,4},{4,5},{5,6},{6,7},{7,0},{8,9},{9,10},{10,1... | collective-permute-start | bytes 8650760 | tf_op jit(solution)/shard_map/ppermute | solution.py:238
  584.6 236.6 %copy-start.24 = (f32[8,1,256]{2,1,0:T(1,128)}, f32[8,1,256]{2,1,0:T(1,128)S(1)}, u32[]{:S(2)}) copy-start(f32[8,1,256]{2,1,0:T(1,128)S(1)} %convert_element_type.149) | copy-start | bytes 24580
  668.1 153.1 %copy-start.22 = (f32[8,1,256]{2,1,0:T(1,128)}, f32[8,1,256]{2,1,0:T(1,128)S(1)}, u32[]{:S(2)}) copy-start(f32[8,1,256]{2,1,0:T(1,128)S(1)} %convert_element_type.148) | copy-start | bytes 24580
  668.7 152.5 %copy-start.39 = (f32[8]{0:T(128)}, f32[8]{0:T(128)S(1)}, u32[]{:S(2)}) copy-start(f32[8]{0:T(128)S(1)} %multiply_power_fusion) | copy-start | bytes 100
  669.8 151.4 %copy-start.30 = (f32[256]{0:T(256)}, f32[256]{0:T(256)S(1)}, u32[]{:S(2)}) copy-start(f32[256]{0:T(256)S(1)} %broadcast_multiply_fusion.5) | copy-start | bytes 3076
  670.2 151.0 %copy-start.32 = (f32[256]{0:T(256)}, f32[256]{0:T(256)S(1)}, u32[]{:S(2)}) copy-start(f32[256]{0:T(256)S(1)} %add_rsqrt_fusion.1) | copy-start | bytes 3076
  670.4 236.8 %collective-permute-start.3 = (bf16[704,2048]{1,0:T(8,128)(2,1)}, bf16[704,2048]{1,0:T(8,128)(2,1)}, u32[]{:S(2)}, u32[]{:S(2)}) collective-permute-start(bf16[704,2048]{1,0:T(8,128)(2,1)} %collective-permute-done.1), channel_id=1, source_target_pairs={{0,7},{1,0},{2,1},{3,2},{4,3},{5,4},{6,5},{7,6},{8,15},{9,8},{10,9... | collective-permute-start | bytes 8650760 | tf_op jit(solution)/shard_map/ppermute | solution.py:247
  670.4 244.8 %collective-permute-start.4 = (bf16[704,2048]{1,0:T(8,128)(2,1)}, bf16[704,2048]{1,0:T(8,128)(2,1)}, u32[]{:S(2)}, u32[]{:S(2)}) collective-permute-start(bf16[704,2048]{1,0:T(8,128)(2,1)} %collective-permute-done.2), channel_id=1, source_target_pairs={{0,1},{1,2},{2,3},{3,4},{4,5},{5,6},{6,7},{7,0},{8,9},{9,10},{10,1... | collective-permute-start | bytes 8650760 | tf_op jit(solution)/shard_map/ppermute | solution.py:238
  835.0 35.2 copy-start.47
  835.0 54.1 %copy-start.42 = (s32[1,256]{1,0:T(1,128)S(1)}, s32[1,256]{1,0:T(1,128)}, u32[]{:S(2)}) copy-start(s32[1,256]{1,0:T(1,128)} %param.20) | copy-start | bytes 3076
  835.0 81.8 %all-to-all-start = ((bf16[256,3,4,512]{0,3,1,2:T(8,128)(2,1)}), bf16[256,3,4,512]{0,3,1,2:T(8,128)(2,1)S(1)}, u32[]{:S(2)}, u32[]{:S(2)}) async-start(bf16[256,3,4,512]{0,3,1,2:T(8,128)(2,1)} %copy.117), calls=%async_computation | async-start | bytes 6291456 | tf_op jit(solution)/shard_map/all_to_all | solution.py:207
  907.1 211.4 %collective-permute-start.5 = (bf16[704,2048]{1,0:T(8,128)(2,1)}, bf16[704,2048]{1,0:T(8,128)(2,1)}, u32[]{:S(2)}, u32[]{:S(2)}) collective-permute-start(bf16[704,2048]{1,0:T(8,128)(2,1)} %collective-permute-done.3), channel_id=1, source_target_pairs={{0,7},{1,0},{2,1},{3,2},{4,3},{5,4},{6,5},{7,6},{8,15},{9,8},{10,9... | collective-permute-start | bytes 8650760 | tf_op jit(solution)/shard_map/ppermute | solution.py:247
  915.3 207.0 %collective-permute-start.6 = (bf16[704,2048]{1,0:T(8,128)(2,1)}, bf16[704,2048]{1,0:T(8,128)(2,1)}, u32[]{:S(2)}, u32[]{:S(2)}) collective-permute-start(bf16[704,2048]{1,0:T(8,128)(2,1)} %collective-permute-done.4), channel_id=1, source_target_pairs={{0,1},{1,2},{2,3},{3,4},{4,5},{5,6},{6,7},{7,0},{8,9},{9,10},{10,1... | collective-permute-start | bytes 8650760 | tf_op jit(solution)/shard_map/ppermute | solution.py:238
  990.2 135.9 %all-to-all-start.1 = ((bf16[4,2,65536]{2,1,0:T(2,128)(2,1)}), bf16[4,2,65536]{2,1,0:T(2,128)(2,1)S(1)}, u32[]{:S(2)}, u32[]{:S(2)}) async-start(bf16[4,2,65536]{2,1,0:T(2,128)(2,1)} %reshape.486), calls=%async_computation.1 | async-start | bytes 2097152 | tf_op jit(solution)/shard_map/all_to_all | solution.py:215
  993.7 2620.0 %reduce-scatter.7.cloned.1.call-start = ((), (), s32[]{:S(2)}) async-start(), calls=%async_computation.11 | async-start | bytes 77856768
  1130.8 781.1 %copy-start.14 = (f32[8,1,256]{2,1,0:T(1,128)S(1)}, f32[8,1,256]{2,1,0:T(1,128)}, u32[]{:S(2)}) copy-start(f32[8,1,256]{2,1,0:T(1,128)} %convert_element_type.151) | copy-start | bytes 24580
  1130.8 781.1 %copy-start.15 = (f32[8,1,256]{2,1,0:T(1,128)S(1)}, f32[8,1,256]{2,1,0:T(1,128)}, u32[]{:S(2)}) copy-start(f32[8,1,256]{2,1,0:T(1,128)} %convert_element_type.152) | copy-start | bytes 24580
  2561.2 18.1 all-to-all-start.2
  2761.1 53.3 %all-to-all-start.3 = ((bf16[1024,3,1,512]{3,1,2,0:T(4,128)(2,1)}), bf16[1024,3,1,512]{3,1,2,0:T(4,128)(2,1)}, u32[]{:S(2)}, u32[]{:S(2)}) async-start(bf16[1024,3,1,512]{3,1,2,0:T(4,128)(2,1)} %copy.126), calls=%async_computation.3 | async-start | bytes 8388608 | tf_op jit(solution)/shard_map/all_to_all | solution.py:312
  2766.2 1389.9 %reduce-scatter.5.cloned.1.call-start = ((), (), s32[]{:S(2)}) async-start(), calls=%async_computation.10 | async-start | bytes 37748736 | tf_op jit(solution)/shard_map/reduce_scatter | solution.py:140
  2861.7 1535.8 %all-reduce.4.cloned.1.call-start = ((), (), s32[]{:S(2)}) async-start(), calls=%async_computation.12 | async-start | bytes 27262976 | tf_op jit(solution)/shard_map/psum | solution.py:328
  (42 other events, 429.9 us)
Sparse Core Ops, SparseCore 0:
  9.5 798.1 all-gather.9
  809.9 220.9 all-gather.11
  1033.0 878.7 all-gather.13
  1913.2 441.0 all-gather.15
  2528.5 1085.1 reduce-scatter.6
  3617.3 538.7 reduce-scatter.4
  4159.3 238.1 all-reduce.3
